TPU v7x, 32 devices: a whole 2x2x4 slice. The times are simulated.
32 devices in a mesh: patch: 8 (over z, y), sub: 4 (over x, core).
Axes of the slice: x: 2, y: 2, z: 4, core: 2. Of those that a mesh axis runs over, the one named last changes fastest.
Arguments:
- sources: int32 [128, 2], replicated, may hold values from 0 to 16383
- diag_coef: float32 [16384], P(('patch', 'sub')), may hold values from 1 to 2
- tiles: float32 [128, 6, 128, 128], P(('patch', 'sub')), may hold values from -0.109375 to 0.109375
- tile_cols: int32 [128, 6], P(('patch', 'sub')), may hold values from 0 to 7
- send_rows: int32 [32, 4, 128], P(('patch', 'sub')), may hold values from 0 to 511
- recv_rows: int32 [32, 512], P(('patch', 'sub')), may hold values from 0 to 511, each once within a row
- bounds: float32 [2], replicated, may hold values from 0.3 to 3.2, as said below
Outputs:
- solution: float32 [16384, 128], P(('patch', 'sub'))
- res_norm: float32 [128], replicated
Inputs may be any that keep to these rules, and one draw needn't show every extreme that they name: bounds[0] lies in 0.3 to 0.5 and bounds[1] in 2.6 to 3.2.
All inputs are finite; a program needn't handle non-finite values.
Results may differ from a plain program's by a relative error of at most 0.0001.
Values sent between devices are 32-bit elements; how exact they have to be, the bound alone decides.
A program may use at most 64 MiB of HBM per device.

v0:
```python
import jax
import jax.numpy as jnp
from jax import lax
from jax.sharding import PartitionSpec as P

ITERS = 8


def shifted(value, axis, steps):
    count = lax.axis_size(axis)
    pairs = [(source, (source + steps) % count) for source in range(count)]
    return lax.ppermute(value, axis, pairs)


def on_device(sources, diag_coef, tiles, tile_cols, send_rows, recv_rows, bounds):
    rows = diag_coef.shape[0]
    columns = sources.shape[0]
    blk_rows = tiles.shape[0]
    per_row = tiles.shape[1]
    tile_size = tiles.shape[2]
    sends = send_rows[0]
    receives = recv_rows[0]
    device = lax.axis_index("patch") * lax.axis_size("sub") + lax.axis_index("sub")
    local_ids = sources - device * rows
    inside = (local_ids >= 0) & (local_ids < rows)
    which = jnp.arange(columns, dtype=jnp.int32)[:, None]
    flat_index = jnp.where(inside, local_ids * columns + which, rows * columns).reshape(-1)
    counts = jax.ops.segment_sum(
        jnp.ones(flat_index.shape, jnp.float32), flat_index, num_segments=rows * columns + 1
    )
    right_side = counts[: rows * columns].reshape(rows, columns)

    def operate(field):
        packed = field[sends]
        below_patch = shifted(packed[1], "patch", 1)
        above_patch = shifted(packed[0], "patch", -1)
        below_sub = shifted(packed[3], "sub", 1)
        above_sub = shifted(packed[2], "sub", -1)
        received = jnp.concatenate([below_patch, above_patch, below_sub, above_sub], axis=0)
        halo_rows = received[receives]
        extended = jnp.concatenate([field, halo_rows], axis=0).reshape(-1, tile_size, columns)
        summed = jnp.zeros((blk_rows, tile_size, columns), jnp.float32)
        for slot_index in range(per_row):
            summed = summed + jnp.einsum(
                "bij,bjk->bik",
                tiles[:, slot_index],
                extended[tile_cols[:, slot_index]],
                precision=lax.Precision.HIGHEST,
            )
        return diag_coef[:, None] * field + summed.reshape(rows, columns)

    centre = (bounds[0] + bounds[1]) / 2.0
    half_width = (bounds[1] - bounds[0]) / 2.0
    ratio = centre / half_width
    damping = 1.0 / ratio
    solution = jnp.zeros_like(right_side)
    residual = right_side
    direction = right_side / centre
    for iteration in range(ITERS):
        solution = solution + direction
        residual = residual - operate(direction)
        if iteration + 1 < ITERS:
            damping_next = 1.0 / (2.0 * ratio - damping)
            direction = (
                damping_next * damping * direction + 2.0 * damping_next / half_width * residual
            )
            damping = damping_next
    final = right_side - operate(solution)
    squares = lax.psum(jnp.sum(final * final, axis=0), ("patch", "sub"))
    return (solution, jnp.sqrt(squares))


def solution(mesh):
    return jax.shard_map(
        on_device,
        mesh=mesh,
        in_specs=(
            P(),
            P(("patch", "sub")),
            P(("patch", "sub"), None, None, None),
            P(("patch", "sub"), None),
            P(("patch", "sub"), None, None),
            P(("patch", "sub"), None),
            P(),
        ),
        out_specs=(P(("patch", "sub"), None), P()),
        check_vma=False,
    )
```

profile of v0, /device:TPU:0, one launch (start us, length us, event | category | flops | bytes accessed | tf_op | source)
XLA Modules:
  0.0 229.8 jit_solution(4072987159246424181)
XLA Ops:
  4.9 2.3 %scatter_custom_fusion = f32[65537]{0:T(1024)S(1)} fusion(s32[256]{0:T(256)S(1)} %reshape.649, f32[256]{0:T(256)S(1)} %broadcast.65, f32[]{:T(128)} %constant.13.clone.1), kind=kCustom, calls=%fused_computation.254 | custom fusion | flops 256 | bytes 262152 | tf_op jit(solution)/shard_map/scatter-add | solution.py:28
  8.4 3.1 %collective-permute-start = (f32[128,128]{1,0:T(8,128)S(1)}, f32[128,128]{1,0:T(8,128)S(1)}, u32[]{:S(2)}, u32[]{:S(2)}) collective-permute-start(f32[128,128]{1,0:T(8,128)S(1)} %get-tuple-element.42), channel_id=1, source_target_pairs={{0,4},{4,8},{8,12},{12,16},{16,20},{20,24},{24,28},{28,0},{1,5},{5... | collective-permute-start | bytes 196616 | tf_op jit(solution)/shard_map/ppermute | solution.py:12
  11.4 3.1 %collective-permute-start.1 = (f32[128,128]{1,0:T(8,128)S(1)}, f32[128,128]{1,0:T(8,128)S(1)}, u32[]{:S(2)}, u32[]{:S(2)}) collective-permute-start(f32[128,128]{1,0:T(8,128)S(1)} %get-tuple-element.44), channel_id=1, source_target_pairs={{0,28},{4,0},{8,4},{12,8},{16,12},{20,16},{24,20},{28,24},{1,29},{... | collective-permute-start | bytes 196616 | tf_op jit(solution)/shard_map/ppermute | solution.py:12
  14.5 1.7 collective-permute-start.3
  28.8 4.7 %collective-permute-start.5 = (f32[128,128]{1,0:T(8,128)S(1)}, f32[128,128]{1,0:T(8,128)S(1)}, u32[]{:S(2)}, u32[]{:S(2)}) collective-permute-start(f32[128,128]{1,0:T(8,128)S(1)} %get-tuple-element.40), channel_id=1, source_target_pairs={{0,28},{4,0},{8,4},{12,8},{16,12},{20,16},{24,20},{28,24},{1,29},{... | collective-permute-start | bytes 196616 | tf_op jit(solution)/shard_map/ppermute | solution.py:12
  35.7 1.4 collective-permute-done.6
  48.3 1.8 collective-permute-start.10
  50.2 4.7 %collective-permute-start.9 = (f32[128,128]{1,0:T(8,128)S(1)}, f32[128,128]{1,0:T(8,128)S(1)}, u32[]{:S(2)}, u32[]{:S(2)}) collective-permute-start(f32[128,128]{1,0:T(8,128)S(1)} %get-tuple-element.36), channel_id=1, source_target_pairs={{0,28},{4,0},{8,4},{12,8},{16,12},{20,16},{24,20},{28,24},{1,29},{... | collective-permute-start | bytes 196616 | tf_op jit(solution)/shard_map/ppermute | solution.py:12
  55.0 2.3 collective-permute-done.8
  70.0 4.7 %collective-permute-start.13 = (f32[128,128]{1,0:T(8,128)S(1)}, f32[128,128]{1,0:T(8,128)S(1)}, u32[]{:S(2)}, u32[]{:S(2)}) collective-permute-start(f32[128,128]{1,0:T(8,128)S(1)} %get-tuple-element.32), channel_id=1, source_target_pairs={{0,28},{4,0},{8,4},{12,8},{16,12},{20,16},{24,20},{28,24},{1,29},{... | collective-permute-start | bytes 196616 | tf_op jit(solution)/shard_map/ppermute | solution.py:12
  74.7 1.7 collective-permute-start.15
  77.0 1.4 collective-permute-done.14
  78.5 1.6 gather_fusion.25
  93.3 4.7 %collective-permute-start.17 = (f32[128,128]{1,0:T(8,128)}, f32[128,128]{1,0:T(8,128)S(1)}, u32[]{:S(2)}, u32[]{:S(2)}) collective-permute-start(f32[128,128]{1,0:T(8,128)} %get-tuple-element.28), channel_id=1, source_target_pairs={{0,28},{4,0},{8,4},{12,8},{16,12},{20,16},{24,20},{28,24},{1,29},{... | collective-permute-start | bytes 196616 | tf_op jit(solution)/shard_map/ppermute | solution.py:12
  101.7 1.6 gather_fusion.33
  108.5 1.4 gather_fusion.37
  119.7 4.7 %collective-permute-start.21 = (f32[128,128]{1,0:T(8,128)S(1)}, f32[128,128]{1,0:T(8,128)S(1)}, u32[]{:S(2)}, u32[]{:S(2)}) collective-permute-start(f32[128,128]{1,0:T(8,128)S(1)} %get-tuple-element.24), channel_id=1, source_target_pairs={{0,28},{4,0},{8,4},{12,8},{16,12},{20,16},{24,20},{28,24},{1,29},{... | collective-permute-start | bytes 196616 | tf_op jit(solution)/shard_map/ppermute | solution.py:12
  128.9 1.6 gather_fusion.41
  136.4 1.4 gather_fusion.46
  145.2 4.7 %collective-permute-start.25 = (f32[128,128]{1,0:T(8,128)S(1)}, f32[128,128]{1,0:T(8,128)S(1)}, u32[]{:S(2)}, u32[]{:S(2)}) collective-permute-start(f32[128,128]{1,0:T(8,128)S(1)} %get-tuple-element.20), channel_id=1, source_target_pairs={{0,28},{4,0},{8,4},{12,8},{16,12},{20,16},{24,20},{28,24},{1,29},{... | collective-permute-start | bytes 196616 | tf_op jit(solution)/shard_map/ppermute | solution.py:12
  154.4 1.6 gather_fusion.49
  169.6 4.7 %collective-permute-start.29 = (f32[128,128]{1,0:T(8,128)S(1)}, f32[128,128]{1,0:T(8,128)S(1)}, u32[]{:S(2)}, u32[]{:S(2)}) collective-permute-start(f32[128,128]{1,0:T(8,128)S(1)} %get-tuple-element.16), channel_id=1, source_target_pairs={{0,28},{4,0},{8,4},{12,8},{16,12},{20,16},{24,20},{28,24},{1,29},{... | collective-permute-start | bytes 196616 | tf_op jit(solution)/shard_map/ppermute | solution.py:12
  176.5 1.4 collective-permute-done.30
  190.5 38.8 %psum.7 = f32[128]{0:T(128)S(1)} all-reduce(f32[128]{0:T(128)S(1)} %fusion.58), channel_id=1, replica_groups=mesh['patch'=8,'sub'=4] {'patch','sub'}, use_global_device_ids=true, to_apply=%region_2.3 | all-reduce | flops 128 | bytes 1024 | tf_op jit(solution)/shard_map/psum | solution.py:69
  (289 shorter events, 122.8 us)
Async XLA Ops:
  8.4 9.8 %collective-permute-start = (f32[128,128]{1,0:T(8,128)S(1)}, f32[128,128]{1,0:T(8,128)S(1)}, u32[]{:S(2)}, u32[]{:S(2)}) collective-permute-start(f32[128,128]{1,0:T(8,128)S(1)} %get-tuple-element.42), channel_id=1, source_target_pairs={{0,4},{4,8},{8,12},{12,16},{16,20},{20,24},{24,28},{28,0},{1,5},{5... | collective-permute-start | bytes 196616 | tf_op jit(solution)/shard_map/ppermute | solution.py:12
  11.4 6.7 %collective-permute-start.1 = (f32[128,128]{1,0:T(8,128)S(1)}, f32[128,128]{1,0:T(8,128)S(1)}, u32[]{:S(2)}, u32[]{:S(2)}) collective-permute-start(f32[128,128]{1,0:T(8,128)S(1)} %get-tuple-element.44), channel_id=1, source_target_pairs={{0,28},{4,0},{8,4},{12,8},{16,12},{20,16},{24,20},{28,24},{1,29},{... | collective-permute-start | bytes 196616 | tf_op jit(solution)/shard_map/ppermute | solution.py:12
  14.5 3.7 %collective-permute-start.2 = (f32[128,128]{1,0:T(8,128)S(1)}, f32[128,128]{1,0:T(8,128)S(1)}, u32[]{:S(2)}, u32[]{:S(2)}) collective-permute-start(f32[128,128]{1,0:T(8,128)S(1)} %get-tuple-element.43), channel_id=1, source_target_pairs={{0,1},{1,2},{2,3},{3,0},{4,5},{5,6},{6,7},{7,4},{8,9},{9,10},{10,1... | collective-permute-start | bytes 196616 | tf_op jit(solution)/shard_map/ppermute | solution.py:12
  14.5 3.7 %collective-permute-start.3 = (f32[128,128]{1,0:T(8,128)S(1)}, f32[128,128]{1,0:T(8,128)S(1)}, u32[]{:S(2)}, u32[]{:S(2)}) collective-permute-start(f32[128,128]{1,0:T(8,128)S(1)} %get-tuple-element.45), channel_id=1, source_target_pairs={{0,3},{1,0},{2,1},{3,2},{4,7},{5,4},{6,5},{7,6},{8,11},{9,8},{10,9... | collective-permute-start | bytes 196616 | tf_op jit(solution)/shard_map/ppermute | solution.py:12
  28.7 7.0 %collective-permute-start.4 = (f32[128,128]{1,0:T(8,128)S(1)}, f32[128,128]{1,0:T(8,128)S(1)}, u32[]{:S(2)}, u32[]{:S(2)}) collective-permute-start(f32[128,128]{1,0:T(8,128)S(1)} %get-tuple-element.38), channel_id=1, source_target_pairs={{0,4},{4,8},{8,12},{12,16},{16,20},{20,24},{24,28},{28,0},{1,5},{5... | collective-permute-start | bytes 196616 | tf_op jit(solution)/shard_map/ppermute | solution.py:12
  28.8 7.0 %collective-permute-start.5 = (f32[128,128]{1,0:T(8,128)S(1)}, f32[128,128]{1,0:T(8,128)S(1)}, u32[]{:S(2)}, u32[]{:S(2)}) collective-permute-start(f32[128,128]{1,0:T(8,128)S(1)} %get-tuple-element.40), channel_id=1, source_target_pairs={{0,28},{4,0},{8,4},{12,8},{16,12},{20,16},{24,20},{28,24},{1,29},{... | collective-permute-start | bytes 196616 | tf_op jit(solution)/shard_map/ppermute | solution.py:12
  48.3 6.7 %collective-permute-start.10 = (f32[128,128]{1,0:T(8,128)S(1)}, f32[128,128]{1,0:T(8,128)S(1)}, u32[]{:S(2)}, u32[]{:S(2)}) collective-permute-start(f32[128,128]{1,0:T(8,128)S(1)} %get-tuple-element.35), channel_id=1, source_target_pairs={{0,1},{1,2},{2,3},{3,0},{4,5},{5,6},{6,7},{7,4},{8,9},{9,10},{10,1... | collective-permute-start | bytes 196616 | tf_op jit(solution)/shard_map/ppermute | solution.py:12
  50.1 4.9 %collective-permute-start.11 = (f32[128,128]{1,0:T(8,128)S(1)}, f32[128,128]{1,0:T(8,128)S(1)}, u32[]{:S(2)}, u32[]{:S(2)}) collective-permute-start(f32[128,128]{1,0:T(8,128)S(1)} %get-tuple-element.37), channel_id=1, source_target_pairs={{0,3},{1,0},{2,1},{3,2},{4,7},{5,4},{6,5},{7,6},{8,11},{9,8},{10,9... | collective-permute-start | bytes 196616 | tf_op jit(solution)/shard_map/ppermute | solution.py:12
  50.2 7.1 %collective-permute-start.8 = (f32[128,128]{1,0:T(8,128)S(1)}, f32[128,128]{1,0:T(8,128)S(1)}, u32[]{:S(2)}, u32[]{:S(2)}) collective-permute-start(f32[128,128]{1,0:T(8,128)S(1)} %get-tuple-element.34), channel_id=1, source_target_pairs={{0,4},{4,8},{8,12},{12,16},{16,20},{20,24},{24,28},{28,0},{1,5},{5... | collective-permute-start | bytes 196616 | tf_op jit(solution)/shard_map/ppermute | solution.py:12
  50.2 7.1 %collective-permute-start.9 = (f32[128,128]{1,0:T(8,128)S(1)}, f32[128,128]{1,0:T(8,128)S(1)}, u32[]{:S(2)}, u32[]{:S(2)}) collective-permute-start(f32[128,128]{1,0:T(8,128)S(1)} %get-tuple-element.36), channel_id=1, source_target_pairs={{0,28},{4,0},{8,4},{12,8},{16,12},{20,16},{24,20},{28,24},{1,29},{... | collective-permute-start | bytes 196616 | tf_op jit(solution)/shard_map/ppermute | solution.py:12
  70.0 7.0 %collective-permute-start.12 = (f32[128,128]{1,0:T(8,128)S(1)}, f32[128,128]{1,0:T(8,128)S(1)}, u32[]{:S(2)}, u32[]{:S(2)}) collective-permute-start(f32[128,128]{1,0:T(8,128)S(1)} %get-tuple-element.30), channel_id=1, source_target_pairs={{0,4},{4,8},{8,12},{12,16},{16,20},{20,24},{24,28},{28,0},{1,5},{5... | collective-permute-start | bytes 196616 | tf_op jit(solution)/shard_map/ppermute | solution.py:12
  70.0 7.0 %collective-permute-start.13 = (f32[128,128]{1,0:T(8,128)S(1)}, f32[128,128]{1,0:T(8,128)S(1)}, u32[]{:S(2)}, u32[]{:S(2)}) collective-permute-start(f32[128,128]{1,0:T(8,128)S(1)} %get-tuple-element.32), channel_id=1, source_target_pairs={{0,28},{4,0},{8,4},{12,8},{16,12},{20,16},{24,20},{28,24},{1,29},{... | collective-permute-start | bytes 196616 | tf_op jit(solution)/shard_map/ppermute | solution.py:12
  74.7 3.7 %collective-permute-start.14 = (f32[128,128]{1,0:T(8,128)S(1)}, f32[128,128]{1,0:T(8,128)S(1)}, u32[]{:S(2)}, u32[]{:S(2)}) collective-permute-start(f32[128,128]{1,0:T(8,128)S(1)} %get-tuple-element.31), channel_id=1, source_target_pairs={{0,1},{1,2},{2,3},{3,0},{4,5},{5,6},{6,7},{7,4},{8,9},{9,10},{10,1... | collective-permute-start | bytes 196616 | tf_op jit(solution)/shard_map/ppermute | solution.py:12
  74.7 3.7 %collective-permute-start.15 = (f32[128,128]{1,0:T(8,128)S(1)}, f32[128,128]{1,0:T(8,128)S(1)}, u32[]{:S(2)}, u32[]{:S(2)}) collective-permute-start(f32[128,128]{1,0:T(8,128)S(1)} %get-tuple-element.33), channel_id=1, source_target_pairs={{0,3},{1,0},{2,1},{3,2},{4,7},{5,4},{6,5},{7,6},{8,11},{9,8},{10,9... | collective-permute-start | bytes 196616 | tf_op jit(solution)/shard_map/ppermute | solution.py:12
  93.3 7.2 %collective-permute-start.16 = (f32[128,128]{1,0:T(8,128)}, f32[128,128]{1,0:T(8,128)S(1)}, u32[]{:S(2)}, u32[]{:S(2)}) collective-permute-start(f32[128,128]{1,0:T(8,128)} %get-tuple-element.26), channel_id=1, source_target_pairs={{0,4},{4,8},{8,12},{12,16},{16,20},{20,24},{24,28},{28,0},{1,5},{5... | collective-permute-start | bytes 196616 | tf_op jit(solution)/shard_map/ppermute | solution.py:12
  93.3 7.2 %collective-permute-start.17 = (f32[128,128]{1,0:T(8,128)}, f32[128,128]{1,0:T(8,128)S(1)}, u32[]{:S(2)}, u32[]{:S(2)}) collective-permute-start(f32[128,128]{1,0:T(8,128)} %get-tuple-element.28), channel_id=1, source_target_pairs={{0,28},{4,0},{8,4},{12,8},{16,12},{20,16},{24,20},{28,24},{1,29},{... | collective-permute-start | bytes 196616 | tf_op jit(solution)/shard_map/ppermute | solution.py:12
  98.0 3.7 %collective-permute-start.18 = (f32[128,128]{1,0:T(8,128)S(1)}, f32[128,128]{1,0:T(8,128)S(1)}, u32[]{:S(2)}, u32[]{:S(2)}) collective-permute-start(f32[128,128]{1,0:T(8,128)S(1)} %get-tuple-element.27), channel_id=1, source_target_pairs={{0,1},{1,2},{2,3},{3,0},{4,5},{5,6},{6,7},{7,4},{8,9},{9,10},{10,1... | collective-permute-start | bytes 196616 | tf_op jit(solution)/shard_map/ppermute | solution.py:12
  119.7 7.2 %collective-permute-start.20 = (f32[128,128]{1,0:T(8,128)}, f32[128,128]{1,0:T(8,128)S(1)}, u32[]{:S(2)}, u32[]{:S(2)}) collective-permute-start(f32[128,128]{1,0:T(8,128)} %get-tuple-element.22), channel_id=1, source_target_pairs={{0,4},{4,8},{8,12},{12,16},{16,20},{20,24},{24,28},{28,0},{1,5},{5... | collective-permute-start | bytes 196616 | tf_op jit(solution)/shard_map/ppermute | solution.py:12
  119.7 7.2 %collective-permute-start.21 = (f32[128,128]{1,0:T(8,128)S(1)}, f32[128,128]{1,0:T(8,128)S(1)}, u32[]{:S(2)}, u32[]{:S(2)}) collective-permute-start(f32[128,128]{1,0:T(8,128)S(1)} %get-tuple-element.24), channel_id=1, source_target_pairs={{0,28},{4,0},{8,4},{12,8},{16,12},{20,16},{24,20},{28,24},{1,29},{... | collective-permute-start | bytes 196616 | tf_op jit(solution)/shard_map/ppermute | solution.py:12
  145.2 7.2 %collective-permute-start.24 = (f32[128,128]{1,0:T(8,128)}, f32[128,128]{1,0:T(8,128)S(1)}, u32[]{:S(2)}, u32[]{:S(2)}) collective-permute-start(f32[128,128]{1,0:T(8,128)} %get-tuple-element.18), channel_id=1, source_target_pairs={{0,4},{4,8},{8,12},{12,16},{16,20},{20,24},{24,28},{28,0},{1,5},{5... | collective-permute-start | bytes 196616 | tf_op jit(solution)/shard_map/ppermute | solution.py:12
  145.2 7.2 %collective-permute-start.25 = (f32[128,128]{1,0:T(8,128)S(1)}, f32[128,128]{1,0:T(8,128)S(1)}, u32[]{:S(2)}, u32[]{:S(2)}) collective-permute-start(f32[128,128]{1,0:T(8,128)S(1)} %get-tuple-element.20), channel_id=1, source_target_pairs={{0,28},{4,0},{8,4},{12,8},{16,12},{20,16},{24,20},{28,24},{1,29},{... | collective-permute-start | bytes 196616 | tf_op jit(solution)/shard_map/ppermute | solution.py:12
  169.5 7.0 %collective-permute-start.28 = (f32[128,128]{1,0:T(8,128)S(1)}, f32[128,128]{1,0:T(8,128)S(1)}, u32[]{:S(2)}, u32[]{:S(2)}) collective-permute-start(f32[128,128]{1,0:T(8,128)S(1)} %get-tuple-element.14), channel_id=1, source_target_pairs={{0,4},{4,8},{8,12},{12,16},{16,20},{20,24},{24,28},{28,0},{1,5},{5... | collective-permute-start | bytes 196616 | tf_op jit(solution)/shard_map/ppermute | solution.py:12
  169.6 7.0 %collective-permute-start.29 = (f32[128,128]{1,0:T(8,128)S(1)}, f32[128,128]{1,0:T(8,128)S(1)}, u32[]{:S(2)}, u32[]{:S(2)}) collective-permute-start(f32[128,128]{1,0:T(8,128)S(1)} %get-tuple-element.16), channel_id=1, source_target_pairs={{0,28},{4,0},{8,4},{12,8},{16,12},{20,16},{24,20},{28,24},{1,29},{... | collective-permute-start | bytes 196616 | tf_op jit(solution)/shard_map/ppermute | solution.py:12
  174.3 3.7 %collective-permute-start.30 = (f32[128,128]{1,0:T(8,128)S(1)}, f32[128,128]{1,0:T(8,128)S(1)}, u32[]{:S(2)}, u32[]{:S(2)}) collective-permute-start(f32[128,128]{1,0:T(8,128)S(1)} %get-tuple-element.15), channel_id=1, source_target_pairs={{0,1},{1,2},{2,3},{3,0},{4,5},{5,6},{6,7},{7,4},{8,9},{9,10},{10,1... | collective-permute-start | bytes 196616 | tf_op jit(solution)/shard_map/ppermute | solution.py:12
  (52 other events, 546.1 us)
where the time goes:
time: 231 us; the launch traced here: 230 us
  local copies, waits for them, and re-layouts  78.7 us (34%)
  starting transfers between devices  53.4 us (23%)
  blocking collectives  38.8 us (17%)
  matrix products  28 us (12%)
  waiting for transfers between devices  13.6 us (6%)
  other arithmetic  11.9 us (5%)
  between operations  5.44 us (2%)
    gather x48, local copies, waits for them, and re-layouts, operate(): extended[tile_cols[:, slot_index]]  54.6 us
    ppermute x32, starting transfers between devices, shifted(): return lax.ppermute(value, axis, pairs)  53.4 us
    psum x1, blocking collectives, on_device(): squares = lax.psum(jnp.sum(final * final, axis=0), ('patch', 'sub'))  38.8 us
    dot_general x48, matrix products, operate(): jnp.einsum('bij,bjk->bik', tiles[:, slot_index], extended[tile_cols[:, sl...  28 us
    ppermute x32, waiting for transfers between devices, shifted(): return lax.ppermute(value, axis, pairs)  13.6 us
    gather x8, local copies, waits for them, and re-layouts, operate(): halo_rows = received[receives]  10.7 us
    gather x8, local copies, waits for them, and re-layouts, operate(): packed = field[sends]  8.28 us
  transfers between devices with their start and end apart: 32, of which 13 were waited for; matrix products, arithmetic and copies ran while one was open for 0% of the time, Pallas kernels for 0%

commit v1 on v0

--- a/solution.py
+++ b/solution.py
@@ -66,7 +66,7 @@
             )
             damping = damping_next
     final = right_side - operate(solution)
-    squares = lax.psum(jnp.sum(final * final, axis=0), ("patch", "sub"))
+    squares = lax.psum(lax.psum(jnp.sum(final * final, axis=0), "sub"), "patch")
     return (solution, jnp.sqrt(squares))
 
 

time: 231 us -> 219 us (0.948)
  blocking collectives: 38.8 us -> 26.9 us
    psum x1 -> x2, blocking collectives: 38.8 us -> 26.9 us  [on_device(): squares = lax.psum(lax.psum(jnp.sum(final * final, axis=0), 'sub'), 'patch')]
where the time goes in v1:
time: 219 us; the launch traced here: 218 us
  local copies, waits for them, and re-layouts  78.9 us (36%)
  starting transfers between devices  53.4 us (24%)
  matrix products  28 us (13%)
  blocking collectives  26.9 us (12%)
  waiting for transfers between devices  13.6 us (6%)
  other arithmetic  11.9 us (5%)
  between operations  5.44 us (2%)
    gather x48, local copies, waits for them, and re-layouts, operate(): extended[tile_cols[:, slot_index]]  54.8 us
    ppermute x32, starting transfers between devices, shifted(): return lax.ppermute(value, axis, pairs)  53.4 us
    dot_general x48, matrix products, operate(): jnp.einsum('bij,bjk->bik', tiles[:, slot_index], extended[tile_cols[:, sl...  28 us
    psum x2, blocking collectives, on_device(): squares = lax.psum(lax.psum(jnp.sum(final * final, axis=0), 'sub'), 'patch')  26.9 us
    ppermute x32, waiting for transfers between devices, shifted(): return lax.ppermute(value, axis, pairs)  13.6 us
    gather x8, local copies, waits for them, and re-layouts, operate(): halo_rows = received[receives]  10.7 us
    gather x8, local copies, waits for them, and re-layouts, operate(): packed = field[sends]  8.28 us
  transfers between devices with their start and end apart: 32, of which 13 were waited for; matrix products, arithmetic and copies ran while one was open for 0% of the time, Pallas kernels for 0%

profile of v1, /device:TPU:0, one launch (start us, length us, event | category | flops | bytes accessed | tf_op | source)
XLA Modules:
  0.0 218.1 jit_solution(14049678176131938214)
XLA Ops:
  4.9 2.3 %scatter_custom_fusion = f32[65537]{0:T(1024)S(1)} fusion(s32[256]{0:T(256)S(1)} %reshape.649, f32[256]{0:T(256)S(1)} %broadcast.65, f32[]{:T(128)} %constant.13.clone.1), kind=kCustom, calls=%fused_computation.254 | custom fusion | flops 256 | bytes 262152 | tf_op jit(solution)/shard_map/scatter-add | solution.py:28
  8.4 3.1 %collective-permute-start = (f32[128,128]{1,0:T(8,128)S(1)}, f32[128,128]{1,0:T(8,128)S(1)}, u32[]{:S(2)}, u32[]{:S(2)}) collective-permute-start(f32[128,128]{1,0:T(8,128)S(1)} %get-tuple-element.42), channel_id=1, source_target_pairs={{0,4},{4,8},{8,12},{12,16},{16,20},{20,24},{24,28},{28,0},{1,5},{5... | collective-permute-start | bytes 196616 | tf_op jit(solution)/shard_map/ppermute | solution.py:12
  11.4 3.1 %collective-permute-start.1 = (f32[128,128]{1,0:T(8,128)S(1)}, f32[128,128]{1,0:T(8,128)S(1)}, u32[]{:S(2)}, u32[]{:S(2)}) collective-permute-start(f32[128,128]{1,0:T(8,128)S(1)} %get-tuple-element.44), channel_id=1, source_target_pairs={{0,28},{4,0},{8,4},{12,8},{16,12},{20,16},{24,20},{28,24},{1,29},{... | collective-permute-start | bytes 196616 | tf_op jit(solution)/shard_map/ppermute | solution.py:12
  14.5 1.7 collective-permute-start.3
  28.8 4.7 %collective-permute-start.5 = (f32[128,128]{1,0:T(8,128)S(1)}, f32[128,128]{1,0:T(8,128)S(1)}, u32[]{:S(2)}, u32[]{:S(2)}) collective-permute-start(f32[128,128]{1,0:T(8,128)S(1)} %get-tuple-element.40), channel_id=1, source_target_pairs={{0,28},{4,0},{8,4},{12,8},{16,12},{20,16},{24,20},{28,24},{1,29},{... | collective-permute-start | bytes 196616 | tf_op jit(solution)/shard_map/ppermute | solution.py:12
  35.7 1.4 collective-permute-done.6
  48.4 1.8 collective-permute-start.10
  50.2 4.7 %collective-permute-start.9 = (f32[128,128]{1,0:T(8,128)S(1)}, f32[128,128]{1,0:T(8,128)S(1)}, u32[]{:S(2)}, u32[]{:S(2)}) collective-permute-start(f32[128,128]{1,0:T(8,128)S(1)} %get-tuple-element.36), channel_id=1, source_target_pairs={{0,28},{4,0},{8,4},{12,8},{16,12},{20,16},{24,20},{28,24},{1,29},{... | collective-permute-start | bytes 196616 | tf_op jit(solution)/shard_map/ppermute | solution.py:12
  55.1 2.3 %collective-permute-done.8 = f32[128,128]{1,0:T(8,128)S(1)} collective-permute-done((f32[128,128]{1,0:T(8,128)S(1)}, f32[128,128]{1,0:T(8,128)S(1)}, u32[]{:S(2)}, u32[]{:S(2)}) %collective-permute-start.8) | collective-permute-done | bytes 65568 | tf_op jit(solution)/shard_map/ppermute | solution.py:12
  70.1 4.7 %collective-permute-start.13 = (f32[128,128]{1,0:T(8,128)S(1)}, f32[128,128]{1,0:T(8,128)S(1)}, u32[]{:S(2)}, u32[]{:S(2)}) collective-permute-start(f32[128,128]{1,0:T(8,128)S(1)} %get-tuple-element.32), channel_id=1, source_target_pairs={{0,28},{4,0},{8,4},{12,8},{16,12},{20,16},{24,20},{28,24},{1,29},{... | collective-permute-start | bytes 196616 | tf_op jit(solution)/shard_map/ppermute | solution.py:12
  74.8 1.7 collective-permute-start.15
  77.0 1.4 collective-permute-done.14
  78.5 1.6 gather_fusion.25
  93.4 4.7 %collective-permute-start.17 = (f32[128,128]{1,0:T(8,128)}, f32[128,128]{1,0:T(8,128)S(1)}, u32[]{:S(2)}, u32[]{:S(2)}) collective-permute-start(f32[128,128]{1,0:T(8,128)} %get-tuple-element.28), channel_id=1, source_target_pairs={{0,28},{4,0},{8,4},{12,8},{16,12},{20,16},{24,20},{28,24},{1,29},{... | collective-permute-start | bytes 196616 | tf_op jit(solution)/shard_map/ppermute | solution.py:12
  101.8 1.6 gather_fusion.33
  108.6 1.4 gather_fusion.37
  119.7 4.7 %collective-permute-start.21 = (f32[128,128]{1,0:T(8,128)S(1)}, f32[128,128]{1,0:T(8,128)S(1)}, u32[]{:S(2)}, u32[]{:S(2)}) collective-permute-start(f32[128,128]{1,0:T(8,128)S(1)} %get-tuple-element.24), channel_id=1, source_target_pairs={{0,28},{4,0},{8,4},{12,8},{16,12},{20,16},{24,20},{28,24},{1,29},{... | collective-permute-start | bytes 196616 | tf_op jit(solution)/shard_map/ppermute | solution.py:12
  129.0 1.6 gather_fusion.41
  145.3 4.7 %collective-permute-start.25 = (f32[128,128]{1,0:T(8,128)S(1)}, f32[128,128]{1,0:T(8,128)S(1)}, u32[]{:S(2)}, u32[]{:S(2)}) collective-permute-start(f32[128,128]{1,0:T(8,128)S(1)} %get-tuple-element.20), channel_id=1, source_target_pairs={{0,28},{4,0},{8,4},{12,8},{16,12},{20,16},{24,20},{28,24},{1,29},{... | collective-permute-start | bytes 196616 | tf_op jit(solution)/shard_map/ppermute | solution.py:12
  154.6 1.6 gather_fusion.49
  169.7 4.7 %collective-permute-start.29 = (f32[128,128]{1,0:T(8,128)S(1)}, f32[128,128]{1,0:T(8,128)S(1)}, u32[]{:S(2)}, u32[]{:S(2)}) collective-permute-start(f32[128,128]{1,0:T(8,128)S(1)} %get-tuple-element.16), channel_id=1, source_target_pairs={{0,28},{4,0},{8,4},{12,8},{16,12},{20,16},{24,20},{28,24},{1,29},{... | collective-permute-start | bytes 196616 | tf_op jit(solution)/shard_map/ppermute | solution.py:12
  176.6 1.4 collective-permute-done.30
  190.7 7.4 %psum.14 = f32[128]{0:T(128)S(1)} all-reduce(f32[128]{0:T(128)S(1)} %fusion.58), channel_id=1, replica_groups=mesh['patch'=8,'sub'=4] {'sub'}, use_global_device_ids=true, to_apply=%region_2.3 | all-reduce | flops 128 | bytes 1024 | tf_op jit(solution)/shard_map/psum | solution.py:69
  198.1 19.5 %psum.15 = f32[128]{0:T(128)S(1)} all-reduce(f32[128]{0:T(128)S(1)} %psum.14), channel_id=1, replica_groups=mesh['patch'=8,'sub'=4] {'patch'}, use_global_device_ids=true, to_apply=%region_3.4 | all-reduce | flops 128 | bytes 1024 | tf_op jit(solution)/shard_map/psum | solution.py:69
  (290 shorter events, 124.4 us)
Async XLA Ops:
  8.4 9.8 %collective-permute-start = (f32[128,128]{1,0:T(8,128)S(1)}, f32[128,128]{1,0:T(8,128)S(1)}, u32[]{:S(2)}, u32[]{:S(2)}) collective-permute-start(f32[128,128]{1,0:T(8,128)S(1)} %get-tuple-element.42), channel_id=1, source_target_pairs={{0,4},{4,8},{8,12},{12,16},{16,20},{20,24},{24,28},{28,0},{1,5},{5... | collective-permute-start | bytes 196616 | tf_op jit(solution)/shard_map/ppermute | solution.py:12
  11.4 6.7 %collective-permute-start.1 = (f32[128,128]{1,0:T(8,128)S(1)}, f32[128,128]{1,0:T(8,128)S(1)}, u32[]{:S(2)}, u32[]{:S(2)}) collective-permute-start(f32[128,128]{1,0:T(8,128)S(1)} %get-tuple-element.44), channel_id=1, source_target_pairs={{0,28},{4,0},{8,4},{12,8},{16,12},{20,16},{24,20},{28,24},{1,29},{... | collective-permute-start | bytes 196616 | tf_op jit(solution)/shard_map/ppermute | solution.py:12
  14.5 3.7 %collective-permute-start.2 = (f32[128,128]{1,0:T(8,128)S(1)}, f32[128,128]{1,0:T(8,128)S(1)}, u32[]{:S(2)}, u32[]{:S(2)}) collective-permute-start(f32[128,128]{1,0:T(8,128)S(1)} %get-tuple-element.43), channel_id=1, source_target_pairs={{0,1},{1,2},{2,3},{3,0},{4,5},{5,6},{6,7},{7,4},{8,9},{9,10},{10,1... | collective-permute-start | bytes 196616 | tf_op jit(solution)/shard_map/ppermute | solution.py:12
  14.5 3.7 %collective-permute-start.3 = (f32[128,128]{1,0:T(8,128)S(1)}, f32[128,128]{1,0:T(8,128)S(1)}, u32[]{:S(2)}, u32[]{:S(2)}) collective-permute-start(f32[128,128]{1,0:T(8,128)S(1)} %get-tuple-element.45), channel_id=1, source_target_pairs={{0,3},{1,0},{2,1},{3,2},{4,7},{5,4},{6,5},{7,6},{8,11},{9,8},{10,9... | collective-permute-start | bytes 196616 | tf_op jit(solution)/shard_map/ppermute | solution.py:12
  28.7 7.0 %collective-permute-start.4 = (f32[128,128]{1,0:T(8,128)S(1)}, f32[128,128]{1,0:T(8,128)S(1)}, u32[]{:S(2)}, u32[]{:S(2)}) collective-permute-start(f32[128,128]{1,0:T(8,128)S(1)} %get-tuple-element.38), channel_id=1, source_target_pairs={{0,4},{4,8},{8,12},{12,16},{16,20},{20,24},{24,28},{28,0},{1,5},{5... | collective-permute-start | bytes 196616 | tf_op jit(solution)/shard_map/ppermute | solution.py:12
  28.8 7.0 %collective-permute-start.5 = (f32[128,128]{1,0:T(8,128)S(1)}, f32[128,128]{1,0:T(8,128)S(1)}, u32[]{:S(2)}, u32[]{:S(2)}) collective-permute-start(f32[128,128]{1,0:T(8,128)S(1)} %get-tuple-element.40), channel_id=1, source_target_pairs={{0,28},{4,0},{8,4},{12,8},{16,12},{20,16},{24,20},{28,24},{1,29},{... | collective-permute-start | bytes 196616 | tf_op jit(solution)/shard_map/ppermute | solution.py:12
  33.5 3.7 %collective-permute-start.6 = (f32[128,128]{1,0:T(8,128)S(1)}, f32[128,128]{1,0:T(8,128)S(1)}, u32[]{:S(2)}, u32[]{:S(2)}) collective-permute-start(f32[128,128]{1,0:T(8,128)S(1)} %get-tuple-element.39), channel_id=1, source_target_pairs={{0,1},{1,2},{2,3},{3,0},{4,5},{5,6},{6,7},{7,4},{8,9},{9,10},{10,1... | collective-permute-start | bytes 196616 | tf_op jit(solution)/shard_map/ppermute | solution.py:12
  48.4 6.7 %collective-permute-start.10 = (f32[128,128]{1,0:T(8,128)S(1)}, f32[128,128]{1,0:T(8,128)S(1)}, u32[]{:S(2)}, u32[]{:S(2)}) collective-permute-start(f32[128,128]{1,0:T(8,128)S(1)} %get-tuple-element.35), channel_id=1, source_target_pairs={{0,1},{1,2},{2,3},{3,0},{4,5},{5,6},{6,7},{7,4},{8,9},{9,10},{10,1... | collective-permute-start | bytes 196616 | tf_op jit(solution)/shard_map/ppermute | solution.py:12
  50.1 4.9 %collective-permute-start.11 = (f32[128,128]{1,0:T(8,128)S(1)}, f32[128,128]{1,0:T(8,128)S(1)}, u32[]{:S(2)}, u32[]{:S(2)}) collective-permute-start(f32[128,128]{1,0:T(8,128)S(1)} %get-tuple-element.37), channel_id=1, source_target_pairs={{0,3},{1,0},{2,1},{3,2},{4,7},{5,4},{6,5},{7,6},{8,11},{9,8},{10,9... | collective-permute-start | bytes 196616 | tf_op jit(solution)/shard_map/ppermute | solution.py:12
  50.2 7.1 %collective-permute-start.8 = (f32[128,128]{1,0:T(8,128)S(1)}, f32[128,128]{1,0:T(8,128)S(1)}, u32[]{:S(2)}, u32[]{:S(2)}) collective-permute-start(f32[128,128]{1,0:T(8,128)S(1)} %get-tuple-element.34), channel_id=1, source_target_pairs={{0,4},{4,8},{8,12},{12,16},{16,20},{20,24},{24,28},{28,0},{1,5},{5... | collective-permute-start | bytes 196616 | tf_op jit(solution)/shard_map/ppermute | solution.py:12
  50.2 7.1 %collective-permute-start.9 = (f32[128,128]{1,0:T(8,128)S(1)}, f32[128,128]{1,0:T(8,128)S(1)}, u32[]{:S(2)}, u32[]{:S(2)}) collective-permute-start(f32[128,128]{1,0:T(8,128)S(1)} %get-tuple-element.36), channel_id=1, source_target_pairs={{0,28},{4,0},{8,4},{12,8},{16,12},{20,16},{24,20},{28,24},{1,29},{... | collective-permute-start | bytes 196616 | tf_op jit(solution)/shard_map/ppermute | solution.py:12
  70.0 7.0 %collective-permute-start.12 = (f32[128,128]{1,0:T(8,128)S(1)}, f32[128,128]{1,0:T(8,128)S(1)}, u32[]{:S(2)}, u32[]{:S(2)}) collective-permute-start(f32[128,128]{1,0:T(8,128)S(1)} %get-tuple-element.30), channel_id=1, source_target_pairs={{0,4},{4,8},{8,12},{12,16},{16,20},{20,24},{24,28},{28,0},{1,5},{5... | collective-permute-start | bytes 196616 | tf_op jit(solution)/shard_map/ppermute | solution.py:12
  70.1 7.0 %collective-permute-start.13 = (f32[128,128]{1,0:T(8,128)S(1)}, f32[128,128]{1,0:T(8,128)S(1)}, u32[]{:S(2)}, u32[]{:S(2)}) collective-permute-start(f32[128,128]{1,0:T(8,128)S(1)} %get-tuple-element.32), channel_id=1, source_target_pairs={{0,28},{4,0},{8,4},{12,8},{16,12},{20,16},{24,20},{28,24},{1,29},{... | collective-permute-start | bytes 196616 | tf_op jit(solution)/shard_map/ppermute | solution.py:12
  74.8 3.7 %collective-permute-start.14 = (f32[128,128]{1,0:T(8,128)S(1)}, f32[128,128]{1,0:T(8,128)S(1)}, u32[]{:S(2)}, u32[]{:S(2)}) collective-permute-start(f32[128,128]{1,0:T(8,128)S(1)} %get-tuple-element.31), channel_id=1, source_target_pairs={{0,1},{1,2},{2,3},{3,0},{4,5},{5,6},{6,7},{7,4},{8,9},{9,10},{10,1... | collective-permute-start | bytes 196616 | tf_op jit(solution)/shard_map/ppermute | solution.py:12
  74.8 3.7 %collective-permute-start.15 = (f32[128,128]{1,0:T(8,128)S(1)}, f32[128,128]{1,0:T(8,128)S(1)}, u32[]{:S(2)}, u32[]{:S(2)}) collective-permute-start(f32[128,128]{1,0:T(8,128)S(1)} %get-tuple-element.33), channel_id=1, source_target_pairs={{0,3},{1,0},{2,1},{3,2},{4,7},{5,4},{6,5},{7,6},{8,11},{9,8},{10,9... | collective-permute-start | bytes 196616 | tf_op jit(solution)/shard_map/ppermute | solution.py:12
  93.4 7.2 %collective-permute-start.16 = (f32[128,128]{1,0:T(8,128)}, f32[128,128]{1,0:T(8,128)S(1)}, u32[]{:S(2)}, u32[]{:S(2)}) collective-permute-start(f32[128,128]{1,0:T(8,128)} %get-tuple-element.26), channel_id=1, source_target_pairs={{0,4},{4,8},{8,12},{12,16},{16,20},{20,24},{24,28},{28,0},{1,5},{5... | collective-permute-start | bytes 196616 | tf_op jit(solution)/shard_map/ppermute | solution.py:12
  93.4 7.2 %collective-permute-start.17 = (f32[128,128]{1,0:T(8,128)}, f32[128,128]{1,0:T(8,128)S(1)}, u32[]{:S(2)}, u32[]{:S(2)}) collective-permute-start(f32[128,128]{1,0:T(8,128)} %get-tuple-element.28), channel_id=1, source_target_pairs={{0,28},{4,0},{8,4},{12,8},{16,12},{20,16},{24,20},{28,24},{1,29},{... | collective-permute-start | bytes 196616 | tf_op jit(solution)/shard_map/ppermute | solution.py:12
  98.1 3.7 %collective-permute-start.18 = (f32[128,128]{1,0:T(8,128)S(1)}, f32[128,128]{1,0:T(8,128)S(1)}, u32[]{:S(2)}, u32[]{:S(2)}) collective-permute-start(f32[128,128]{1,0:T(8,128)S(1)} %get-tuple-element.27), channel_id=1, source_target_pairs={{0,1},{1,2},{2,3},{3,0},{4,5},{5,6},{6,7},{7,4},{8,9},{9,10},{10,1... | collective-permute-start | bytes 196616 | tf_op jit(solution)/shard_map/ppermute | solution.py:12
  119.7 7.2 %collective-permute-start.20 = (f32[128,128]{1,0:T(8,128)}, f32[128,128]{1,0:T(8,128)S(1)}, u32[]{:S(2)}, u32[]{:S(2)}) collective-permute-start(f32[128,128]{1,0:T(8,128)} %get-tuple-element.22), channel_id=1, source_target_pairs={{0,4},{4,8},{8,12},{12,16},{16,20},{20,24},{24,28},{28,0},{1,5},{5... | collective-permute-start | bytes 196616 | tf_op jit(solution)/shard_map/ppermute | solution.py:12
  119.7 7.2 %collective-permute-start.21 = (f32[128,128]{1,0:T(8,128)S(1)}, f32[128,128]{1,0:T(8,128)S(1)}, u32[]{:S(2)}, u32[]{:S(2)}) collective-permute-start(f32[128,128]{1,0:T(8,128)S(1)} %get-tuple-element.24), channel_id=1, source_target_pairs={{0,28},{4,0},{8,4},{12,8},{16,12},{20,16},{24,20},{28,24},{1,29},{... | collective-permute-start | bytes 196616 | tf_op jit(solution)/shard_map/ppermute | solution.py:12
  145.3 7.2 %collective-permute-start.24 = (f32[128,128]{1,0:T(8,128)}, f32[128,128]{1,0:T(8,128)S(1)}, u32[]{:S(2)}, u32[]{:S(2)}) collective-permute-start(f32[128,128]{1,0:T(8,128)} %get-tuple-element.18), channel_id=1, source_target_pairs={{0,4},{4,8},{8,12},{12,16},{16,20},{20,24},{24,28},{28,0},{1,5},{5... | collective-permute-start | bytes 196616 | tf_op jit(solution)/shard_map/ppermute | solution.py:12
  145.3 7.2 %collective-permute-start.25 = (f32[128,128]{1,0:T(8,128)S(1)}, f32[128,128]{1,0:T(8,128)S(1)}, u32[]{:S(2)}, u32[]{:S(2)}) collective-permute-start(f32[128,128]{1,0:T(8,128)S(1)} %get-tuple-element.20), channel_id=1, source_target_pairs={{0,28},{4,0},{8,4},{12,8},{16,12},{20,16},{24,20},{28,24},{1,29},{... | collective-permute-start | bytes 196616 | tf_op jit(solution)/shard_map/ppermute | solution.py:12
  169.6 7.0 %collective-permute-start.28 = (f32[128,128]{1,0:T(8,128)S(1)}, f32[128,128]{1,0:T(8,128)S(1)}, u32[]{:S(2)}, u32[]{:S(2)}) collective-permute-start(f32[128,128]{1,0:T(8,128)S(1)} %get-tuple-element.14), channel_id=1, source_target_pairs={{0,4},{4,8},{8,12},{12,16},{16,20},{20,24},{24,28},{28,0},{1,5},{5... | collective-permute-start | bytes 196616 | tf_op jit(solution)/shard_map/ppermute | solution.py:12
  169.7 7.0 %collective-permute-start.29 = (f32[128,128]{1,0:T(8,128)S(1)}, f32[128,128]{1,0:T(8,128)S(1)}, u32[]{:S(2)}, u32[]{:S(2)}) collective-permute-start(f32[128,128]{1,0:T(8,128)S(1)} %get-tuple-element.16), channel_id=1, source_target_pairs={{0,28},{4,0},{8,4},{12,8},{16,12},{20,16},{24,20},{28,24},{1,29},{... | collective-permute-start | bytes 196616 | tf_op jit(solution)/shard_map/ppermute | solution.py:12
  (52 other events, 546.6 us)
